TPU v7x, 256 devices: a whole 4x4x8 slice. The times are simulated.
256 devices in a mesh: bank: 16 (over y, x), zero: 16 (over z, core).
Axes of the slice: x: 4, y: 4, z: 8, core: 2. Of those that a mesh axis runs over, the one named last changes fastest.
Arguments:
- w_down: float32 [64, 1024, 2048], P('bank', None, 'zero'), may hold values from -0.25 to 0.25
- avg_down: bfloat16 [64, 1024, 2048], P('bank', None, 'zero'), may hold values from -0.09375 to 0.09375
- router_weight: float32 [2048, 64], P('zero', 'bank'), may hold values from -0.125 to 0.125
- router_gain: float32 [2048], P('zero'), may hold values from 0.25 to 1.75
Outputs:
- serve_down: bfloat16 [64, 1024, 2048], P('bank')
- scale_down: float32 [64, 1024], P('bank')
- serve_router: bfloat16 [2048, 64], replicated
All inputs are finite; a program needn't handle non-finite values.
Results may differ from a plain program's by a relative error of at most 0.001.
Values may be sent and summed in bfloat16 or wider, within the bound.
No kernel may reach another device: no remote copies, remote signals or barrier semaphores. Data moves between devices by JAX's collectives and lax.ppermute only.
A program may use at most 128 MiB of HBM per device.

v0:
```python
import jax
import jax.numpy as jnp
from jax import lax
from jax.sharding import PartitionSpec as P


def copy_for_each(x, axis):
    copies = jnp.broadcast_to(x, (lax.axis_size(axis), *x.shape))
    return lax.all_to_all(copies, axis, split_axis=0, concat_axis=0, tiled=True)


def over_copies(x, axis):
    return copy_for_each(x, axis).sum(axis=0)


def in_order(parts, dim):
    dims = list(parts.shape[1:])
    dims[dim] *= parts.shape[0]
    return jnp.moveaxis(parts, 0, dim).reshape(dims)


def gather_directly(x, axis, dim):
    parts = copy_for_each(x, axis)
    return in_order(parts, dim)


def shards(w_down, avg_down, router_weight, router_gain):
    fresh_down = w_down + avg_down.astype(jnp.float32)
    total_down = over_copies(jnp.sum(fresh_down * fresh_down, axis=2), "zero")
    scale_down = jnp.sqrt(total_down)
    narrow_down = (fresh_down / jnp.expand_dims(scale_down, 2)).astype(jnp.bfloat16)
    serve_down = lax.all_gather(narrow_down, "zero", axis=2, tiled=True)
    part_router = (router_weight * router_gain[:, None]).astype(jnp.bfloat16)
    row_router = gather_directly(part_router, "zero", 0)
    serve_router = gather_directly(row_router, "bank", 1)
    return (serve_down, scale_down, serve_router)


def solution(mesh):
    return jax.shard_map(
        shards,
        mesh=mesh,
        in_specs=(P("bank", None, "zero"), P("bank", None, "zero"), P("zero", "bank"), P("zero")),
        out_specs=(P("bank", None, None), P("bank", None), P()),
        check_vma=False,
    )
```

profile of v0, /device:TPU:1, one launch (start us, length us, event | category | flops | bytes accessed | tf_op | source)
XLA Modules:
  0.0 152.9 jit_solution(14177765800500866044)
XLA Ops:
  7.2 0.0 copy-start
  7.2 0.0 copy-start.1
  7.2 0.0 all-gather.2.cloned.1.call-start
  7.2 2.6 %multiply_reduce_fusion = f32[4,1024]{1,0:T(4,128)S(1)} fusion(f32[4,1024,128]{2,1,0:T(8,128)} %param.4, bf16[4,1024,128]{2,1,0:T(8,128)(2,1)} %param.5), kind=kLoop, calls=%fused_computation.1 | loop fusion | flops 2093056 | bytes 3162112 | tf_op jit(solution)/shard_map/reduce_sum | solution.py:29
  9.9 21.4 %all_to_all.15 = f32[16,4,1024]{2,1,0:T(4,128)S(1)} all-to-all(f32[16,4,1024]{2,1,0:T(4,128)S(1)} %broadcast_in_dim.11), channel_id=1, replica_groups=mesh['bank'=16,'zero'=16] {'zero'}, dimensions={0} | all-to-all | bytes 524288 | tf_op jit(solution)/shard_map/all_to_all | solution.py:9
  31.3 0.1 reduce_sum.19
  31.3 0.0 copy-done
  31.4 0.0 copy-done.1
  31.4 0.0 copy-start.2
  31.4 0.0 copy-start.3
  31.4 0.0 copy-start.4
  31.4 1.5 divide_convert_fusion
  32.9 0.0 copy-done.2
  32.9 0.0 all-gather.2.cloned.1.call-update
  32.9 0.0 copy-done.3
  33.0 0.0 copy-done.4
  33.0 10.1 %all_to_all.16 = bf16[16,128,4]{1,2,0:T(4,128)(2,1)S(1)} all-to-all(bf16[16,128,4]{1,2,0:T(4,128)(2,1)S(1)} %broadcast_in_dim.12), channel_id=1, replica_groups=mesh['bank'=16,'zero'=16] {'zero'}, dimensions={0} | all-to-all | bytes 32768 | tf_op jit(solution)/shard_map/all_to_all | solution.py:9
  43.1 0.1 broadcast_in_dim.13
  43.2 14.7 %all_to_all.17 = bf16[16,2048,4]{1,2,0:T(4,128)(2,1)S(1)} all-to-all(bf16[16,2048,4]{1,2,0:T(4,128)(2,1)S(1)} %broadcast_in_dim.13), channel_id=1, replica_groups=mesh['bank'=16,'zero'=16] {'bank'}, dimensions={0} | all-to-all | bytes 524288 | tf_op jit(solution)/shard_map/all_to_all | solution.py:9
  57.9 0.8 reshape.17
  58.6 73.3 %all-gather.2.cloned.1.call-done = bf16[4,1024,2048]{2,1,0:T(8,128)(2,1)} async-done(((bf16[4,1024,128]{2,1,0:T(8,128)(2,1)}), bf16[4,1024,2048]{2,1,0:T(8,128)(2,1)}) %all-gather.2.cloned.1.call-update) | async-done | bytes 16777232 | tf_op jit(solution)/shard_map/all_gather | solution.py:32
  131.9 14.2 %copy.10 = bf16[4,1024,2048]{2,1,0:T(8,128)(2,1)} copy(bf16[4,1024,2048]{2,1,0:T(8,128)(2,1)} %all-gather.2.cloned.1.call-done) | data formatting | bytes 33554432
  (4 shorter events, 0.1 us)
Async XLA Ops:
  7.2 24.2 %copy-start = (f32[4,1024,128]{2,1,0:T(8,128)S(1)}, f32[4,1024,128]{2,1,0:T(8,128)}, u32[]{:S(2)}) copy-start(f32[4,1024,128]{2,1,0:T(8,128)} %param.4) | copy-start | bytes 6291460
  7.2 24.2 %copy-start.1 = (bf16[4,1024,128]{2,1,0:T(8,128)(2,1)S(1)}, bf16[4,1024,128]{2,1,0:T(8,128)(2,1)}, u32[]{:S(2)}) copy-start(bf16[4,1024,128]{2,1,0:T(8,128)(2,1)} %param.5) | copy-start | bytes 3145732
  7.2 124.7 %all-gather.2.cloned.1.call-start = ((), (), s32[]{:S(2)}) async-start(), calls=%async_computation.3 | async-start | bytes 17825792 | tf_op jit(solution)/shard_map/all_gather | solution.py:32
  31.4 1.6 %copy-start.2 = (f32[4,1024]{1,0:T(4,128)}, f32[4,1024]{1,0:T(4,128)S(1)}, u32[]{:S(2)}) copy-start(f32[4,1024]{1,0:T(4,128)S(1)} %sqrt.7) | copy-start | bytes 49156
  31.4 1.6 %copy-start.3 = (f32[128,4]{0,1:T(4,128)S(1)}, f32[128,4]{0,1:T(4,128)}, u32[]{:S(2)}) copy-start(f32[128,4]{0,1:T(4,128)} %param.6) | copy-start | bytes 6148
  31.4 1.6 %copy-start.4 = (f32[128]{0:T(128)S(1)}, f32[128]{0:T(128)}, u32[]{:S(2)}) copy-start(f32[128]{0:T(128)} %param.7) | copy-start | bytes 1540
Sparse Core Ops, SparseCore 0:
  33.1 98.8 all-gather.1
where the time goes:
time: 153 us
  waiting for transfers between devices  73.3 us (48%)
  blocking collectives  46.1 us (30%)
  local copies, waits for them, and re-layouts  15.1 us (10%)
  between operations  14.1 us (9%)
  other arithmetic  4.21 us (3%)
    all_gather x1, waiting for transfers between devices, shards(): serve_down = lax.all_gather(narrow_down, 'zero', axis=2, tiled=True)  73.3 us
    all_to_all x3, blocking collectives, copy_for_each(): return lax.all_to_all(copies, axis, split_axis=0, concat_axis=0, tiled=True)  46.1 us
    unnamed x11, local copies, waits for them, and re-layouts  14.2 us
  transfers between devices with their start and end apart: 1, of which 1 were waited for; matrix products, arithmetic and copies ran while one was open for 1% of the time, Pallas kernels for 0%

commit v1 on v0

--- a/solution.py
+++ b/solution.py
@@ -2,6 +2,12 @@
 import jax.numpy as jnp
 from jax import lax
 from jax.sharding import PartitionSpec as P
+
+
+def laid_out(parts, dim):
+    shape = list(parts.shape[1:])
+    shape[dim] *= parts.shape[0]
+    return jnp.moveaxis(parts, 0, dim).reshape(shape)
 
 
 def copy_for_each(x, axis):
@@ -29,7 +35,19 @@
     total_down = over_copies(jnp.sum(fresh_down * fresh_down, axis=2), "zero")
     scale_down = jnp.sqrt(total_down)
     narrow_down = (fresh_down / jnp.expand_dims(scale_down, 2)).astype(jnp.bfloat16)
-    serve_down = lax.all_gather(narrow_down, "zero", axis=2, tiled=True)
+    devices = lax.axis_size("zero")
+    pairs = [(i, (i + 1) % devices) for i in range(devices)]
+    back = [(b, a) for a, b in pairs]
+    lower, upper = ([], [])
+    for step in range(devices - 1):
+        if step % 2 == 0:
+            lower.append(lax.ppermute(lower[-1] if lower else narrow_down, "zero", pairs))
+        else:
+            upper.append(lax.ppermute(upper[-1] if upper else narrow_down, "zero", back))
+    blocks = jnp.stack([*lower[::-1], narrow_down, *upper])
+    shift = lax.axis_index("zero") - len(lower)
+    blocks = blocks[(jnp.arange(devices) - shift) % devices]
+    serve_down = laid_out(blocks, 2)
     part_router = (router_weight * router_gain[:, None]).astype(jnp.bfloat16)
     row_router = gather_directly(part_router, "zero", 0)
     serve_router = gather_directly(row_router, "bank", 1)

time: 153 us -> 224 us (1.46)
  starting transfers between devices: 0.04 us -> 44.7 us
  local copies, waits for them, and re-layouts: 15.1 us -> 57.7 us
  between operations: 14.1 us -> 0.73 us
  waiting for transfers between devices: 73.3 us -> 70.4 us
    all_gather x1 -> x0, waiting for transfers between devices: 73.3 us -> none  [shards(): serve_down = lax.all_gather(narrow_down, 'zero', axis=2, tiled=True)]
    ppermute x0 -> x15, waiting for transfers between devices: none -> 62.3 us  [the longest x8 56.9 us: shards(): lax.ppermute(lower[-1] if lower else narrow_down, 'zero', pairs)]
    ppermute x0 -> x15, starting transfers between devices: none -> 37.9 us  [the longest x7 20.5 us: shards(): lax.ppermute(upper[-1] if upper else narrow_down, 'zero', back)]
    reshape x0 -> x1, local copies, waits for them, and re-layouts: none -> 14.4 us  [laid_out(): return jnp.moveaxis(parts, 0, dim).reshape(shape)]
    unnamed x11 -> x39, local copies, waits for them, and re-layouts: 14.2 us -> 27.6 us
    gather x0 -> x1, local copies, waits for them, and re-layouts: none -> 13 us  [shards(): blocks = blocks[(jnp.arange(devices) - shift) % devices]]
    all_to_all x0 -> x1, waiting for transfers between devices: none -> 8.07 us  [copy_for_each(): return lax.all_to_all(copies, axis, split_axis=0, concat_axis=0, tiled=True)]
    all_to_all x0 -> x1, starting transfers between devices: none -> 6.75 us  [copy_for_each(): return lax.all_to_all(copies, axis, split_axis=0, concat_axis=0, tiled=True)]
  transfers between devices with their start and end apart: 1 -> 16, of which waited for: 1 -> 13; matrix products, arithmetic and copies ran while one was open for 1% -> 13% of each run, Pallas kernels for 0% -> 0%
where the time goes in v1:
time: 224 us; the launch traced here: 223 us
  waiting for transfers between devices  70.4 us (31%)
  local copies, waits for them, and re-layouts  57.7 us (26%)
  starting transfers between devices  44.7 us (20%)
  blocking collectives  44.4 us (20%)
  other arithmetic  5.46 us (2%)
    ppermute x8, waiting for transfers between devices, shards(): lax.ppermute(lower[-1] if lower else narrow_down, 'zero', pairs)  56.9 us
    all_to_all x2, blocking collectives, copy_for_each(): return lax.all_to_all(copies, axis, split_axis=0, concat_axis=0, tiled=True)  44.4 us
    unnamed x39, local copies, waits for them, and re-layouts  27.6 us
    ppermute x7, starting transfers between devices, shards(): lax.ppermute(upper[-1] if upper else narrow_down, 'zero', back)  20.5 us
    ppermute x8, starting transfers between devices, shards(): lax.ppermute(lower[-1] if lower else narrow_down, 'zero', pairs)  17.5 us
    reshape x1, local copies, waits for them, and re-layouts, laid_out(): return jnp.moveaxis(parts, 0, dim).reshape(shape)  14.4 us
    gather x1, local copies, waits for them, and re-layouts, shards(): blocks = blocks[(jnp.arange(devices) - shift) % devices]  13 us
    all_to_all x1, waiting for transfers between devices, copy_for_each(): return lax.all_to_all(copies, axis, split_axis=0, concat_axis=0, tiled=True)  8.07 us
  transfers between devices with their start and end apart: 16, of which 13 were waited for; matrix products, arithmetic and copies ran while one was open for 13% of the time, Pallas kernels for 0%

profile of v1, /device:TPU:1, one launch (start us, length us, event | category | flops | bytes accessed | tf_op | source)
XLA Modules:
  0.0 223.4 jit_solution(8070513788813625847)
XLA Ops:
  3.2 21.4 %all_to_all.15 = f32[16,4,1024]{2,1,0:T(4,128)S(1)} all-to-all(f32[16,4,1024]{2,1,0:T(4,128)S(1)} %broadcast_in_dim.12), channel_id=1, replica_groups=mesh['bank'=16,'zero'=16] {'zero'}, dimensions={0} | all-to-all | bytes 524288 | tf_op jit(solution)/shard_map/all_to_all | solution.py:15
  26.9 11.7 %collective-permute-done = bf16[4,1024,128]{2,1,0:T(8,128)(2,1)S(1)} collective-permute-done((bf16[4,1024,128]{2,1,0:T(8,128)(2,1)S(1)}, bf16[4,1024,128]{2,1,0:T(8,128)(2,1)S(1)}, u32[]{:S(2)}, u32[]{:S(2)}) %collective-permute-start) | collective-permute-done | bytes 1048608 | tf_op jit(solution)/shard_map/ppermute | solution.py:44
  38.6 2.5 %collective-permute-start.1 = (bf16[4,1024,128]{2,1,0:T(8,128)(2,1)S(1)}, bf16[4,1024,128]{2,1,0:T(8,128)(2,1)S(1)}, u32[]{:S(2)}, u32[]{:S(2)}) collective-permute-start(bf16[4,1024,128]{2,1,0:T(8,128)(2,1)S(1)} %collective-permute-done), channel_id=1, source_target_pairs={{0,1},{1,2},{2,3},{3,4},{4,5},{5,6},{6,7},{7,8},{8,9},{9,10},{10,1... | collective-permute-start | bytes 3145736 | tf_op jit(solution)/shard_map/ppermute | solution.py:44
  41.9 10.9 %collective-permute-done.1 = bf16[4,1024,128]{2,1,0:T(8,128)(2,1)S(1)} collective-permute-done((bf16[4,1024,128]{2,1,0:T(8,128)(2,1)S(1)}, bf16[4,1024,128]{2,1,0:T(8,128)(2,1)S(1)}, u32[]{:S(2)}, u32[]{:S(2)}) %collective-permute-start.1) | collective-permute-done | bytes 1048608 | tf_op jit(solution)/shard_map/ppermute | solution.py:44
  52.8 2.5 %collective-permute-start.2 = (bf16[4,1024,128]{2,1,0:T(8,128)(2,1)S(1)}, bf16[4,1024,128]{2,1,0:T(8,128)(2,1)S(1)}, u32[]{:S(2)}, u32[]{:S(2)}) collective-permute-start(bf16[4,1024,128]{2,1,0:T(8,128)(2,1)S(1)} %collective-permute-done.1), channel_id=1, source_target_pairs={{0,1},{1,2},{2,3},{3,4},{4,5},{5,6},{6,7},{7,8},{8,9},{9,10},{10,1... | collective-permute-start | bytes 3145736 | tf_op jit(solution)/shard_map/ppermute | solution.py:44
  57.4 9.6 %collective-permute-done.2 = bf16[4,1024,128]{2,1,0:T(8,128)(2,1)S(1)} collective-permute-done((bf16[4,1024,128]{2,1,0:T(8,128)(2,1)S(1)}, bf16[4,1024,128]{2,1,0:T(8,128)(2,1)S(1)}, u32[]{:S(2)}, u32[]{:S(2)}) %collective-permute-start.2) | collective-permute-done | bytes 1048608 | tf_op jit(solution)/shard_map/ppermute | solution.py:44
  67.0 2.5 %collective-permute-start.3 = (bf16[4,1024,128]{2,1,0:T(8,128)(2,1)S(1)}, bf16[4,1024,128]{2,1,0:T(8,128)(2,1)S(1)}, u32[]{:S(2)}, u32[]{:S(2)}) collective-permute-start(bf16[4,1024,128]{2,1,0:T(8,128)(2,1)S(1)} %collective-permute-done.2), channel_id=1, source_target_pairs={{0,1},{1,2},{2,3},{3,4},{4,5},{5,6},{6,7},{7,8},{8,9},{9,10},{10,1... | collective-permute-start | bytes 3145736 | tf_op jit(solution)/shard_map/ppermute | solution.py:44
  70.1 2.7 %collective-permute-start.10 = (bf16[4,1024,128]{2,1,0:T(8,128)(2,1)S(1)}, bf16[4,1024,128]{2,1,0:T(8,128)(2,1)S(1)}, u32[]{:S(2)}, u32[]{:S(2)}) collective-permute-start(bf16[4,1024,128]{2,1,0:T(8,128)(2,1)S(1)} %collective-permute-done.9), channel_id=1, source_target_pairs={{1,0},{2,1},{3,2},{4,3},{5,4},{6,5},{7,6},{8,7},{9,8},{10,9},{11,1... | collective-permute-start | bytes 3145736 | tf_op jit(solution)/shard_map/ppermute | solution.py:46
  72.9 8.4 %collective-permute-done.3 = bf16[4,1024,128]{2,1,0:T(8,128)(2,1)S(1)} collective-permute-done((bf16[4,1024,128]{2,1,0:T(8,128)(2,1)S(1)}, bf16[4,1024,128]{2,1,0:T(8,128)(2,1)S(1)}, u32[]{:S(2)}, u32[]{:S(2)}) %collective-permute-start.3) | collective-permute-done | bytes 1048608 | tf_op jit(solution)/shard_map/ppermute | solution.py:44
  81.3 2.5 %collective-permute-start.4 = (bf16[4,1024,128]{2,1,0:T(8,128)(2,1)S(1)}, bf16[4,1024,128]{2,1,0:T(8,128)(2,1)S(1)}, u32[]{:S(2)}, u32[]{:S(2)}) collective-permute-start(bf16[4,1024,128]{2,1,0:T(8,128)(2,1)S(1)} %collective-permute-done.3), channel_id=1, source_target_pairs={{0,1},{1,2},{2,3},{3,4},{4,5},{5,6},{6,7},{7,8},{8,9},{9,10},{10,1... | collective-permute-start | bytes 3145736 | tf_op jit(solution)/shard_map/ppermute | solution.py:44
  84.6 3.6 %collective-permute-start.11 = (bf16[4,1024,128]{2,1,0:T(8,128)(2,1)S(1)}, bf16[4,1024,128]{2,1,0:T(8,128)(2,1)S(1)}, u32[]{:S(2)}, u32[]{:S(2)}) collective-permute-start(bf16[4,1024,128]{2,1,0:T(8,128)(2,1)S(1)} %collective-permute-done.10), channel_id=1, source_target_pairs={{1,0},{2,1},{3,2},{4,3},{5,4},{6,5},{7,6},{8,7},{9,8},{10,9},{11,1... | collective-permute-start | bytes 3145736 | tf_op jit(solution)/shard_map/ppermute | solution.py:46
  88.3 7.2 %collective-permute-done.4 = bf16[4,1024,128]{2,1,0:T(8,128)(2,1)S(1)} collective-permute-done((bf16[4,1024,128]{2,1,0:T(8,128)(2,1)S(1)}, bf16[4,1024,128]{2,1,0:T(8,128)(2,1)S(1)}, u32[]{:S(2)}, u32[]{:S(2)}) %collective-permute-start.4) | collective-permute-done | bytes 1048608 | tf_op jit(solution)/shard_map/ppermute | solution.py:44
  95.5 2.5 %collective-permute-start.5 = (bf16[4,1024,128]{2,1,0:T(8,128)(2,1)S(1)}, bf16[4,1024,128]{2,1,0:T(8,128)(2,1)S(1)}, u32[]{:S(2)}, u32[]{:S(2)}) collective-permute-start(bf16[4,1024,128]{2,1,0:T(8,128)(2,1)S(1)} %collective-permute-done.4), channel_id=1, source_target_pairs={{0,1},{1,2},{2,3},{3,4},{4,5},{5,6},{6,7},{7,8},{8,9},{9,10},{10,1... | collective-permute-start | bytes 3145736 | tf_op jit(solution)/shard_map/ppermute | solution.py:44
  100.1 4.6 %collective-permute-start.12 = (bf16[4,1024,128]{2,1,0:T(8,128)(2,1)S(1)}, bf16[4,1024,128]{2,1,0:T(8,128)(2,1)}, u32[]{:S(2)}, u32[]{:S(2)}) collective-permute-start(bf16[4,1024,128]{2,1,0:T(8,128)(2,1)S(1)} %collective-permute-done.11), channel_id=1, source_target_pairs={{1,0},{2,1},{3,2},{4,3},{5,4},{6,5},{7,6},{8,7},{9,8},{10,9},{11,1... | collective-permute-start | bytes 3145736 | tf_op jit(solution)/shard_map/ppermute | solution.py:46
  104.7 5.0 %collective-permute-done.5 = bf16[4,1024,128]{2,1,0:T(8,128)(2,1)S(1)} collective-permute-done((bf16[4,1024,128]{2,1,0:T(8,128)(2,1)S(1)}, bf16[4,1024,128]{2,1,0:T(8,128)(2,1)S(1)}, u32[]{:S(2)}, u32[]{:S(2)}) %collective-permute-start.5) | collective-permute-done | bytes 1048608 | tf_op jit(solution)/shard_map/ppermute | solution.py:44
  109.7 2.5 %collective-permute-start.6 = (bf16[4,1024,128]{2,1,0:T(8,128)(2,1)S(1)}, bf16[4,1024,128]{2,1,0:T(8,128)(2,1)}, u32[]{:S(2)}, u32[]{:S(2)}) collective-permute-start(bf16[4,1024,128]{2,1,0:T(8,128)(2,1)S(1)} %collective-permute-done.5), channel_id=1, source_target_pairs={{0,1},{1,2},{2,3},{3,4},{4,5},{5,6},{6,7},{7,8},{8,9},{9,10},{10,1... | collective-permute-start | bytes 3145736 | tf_op jit(solution)/shard_map/ppermute | solution.py:44
  114.7 5.3 %collective-permute-start.13 = (bf16[4,1024,128]{2,1,0:T(8,128)(2,1)}, bf16[4,1024,128]{2,1,0:T(8,128)(2,1)}, u32[]{:S(2)}, u32[]{:S(2)}) collective-permute-start(bf16[4,1024,128]{2,1,0:T(8,128)(2,1)} %collective-permute-done.12), channel_id=1, source_target_pairs={{1,0},{2,1},{3,2},{4,3},{5,4},{6,5},{7,6},{8,7},{9,8},{10,9},{11,1... | collective-permute-start | bytes 3145736 | tf_op jit(solution)/shard_map/ppermute | solution.py:46
  120.0 4.0 %collective-permute-done.6 = bf16[4,1024,128]{2,1,0:T(8,128)(2,1)} collective-permute-done((bf16[4,1024,128]{2,1,0:T(8,128)(2,1)S(1)}, bf16[4,1024,128]{2,1,0:T(8,128)(2,1)}, u32[]{:S(2)}, u32[]{:S(2)}) %collective-permute-start.6) | collective-permute-done | bytes 1048608 | tf_op jit(solution)/shard_map/ppermute | solution.py:44
  124.0 2.6 %collective-permute-start.7 = (bf16[4,1024,128]{2,1,0:T(8,128)(2,1)}, bf16[4,1024,128]{2,1,0:T(8,128)(2,1)}, u32[]{:S(2)}, u32[]{:S(2)}) collective-permute-start(bf16[4,1024,128]{2,1,0:T(8,128)(2,1)} %collective-permute-done.6), channel_id=1, source_target_pairs={{0,1},{1,2},{2,3},{3,4},{4,5},{5,6},{6,7},{7,8},{8,9},{9,10},{10,1... | collective-permute-start | bytes 3145736 | tf_op jit(solution)/shard_map/ppermute | solution.py:44
  127.2 23.1 %all_to_all.16 = bf16[16,128,4]{1,2,0:T(4,128)(2,1)S(1)} all-to-all(bf16[16,128,4]{1,2,0:T(4,128)(2,1)S(1)} %broadcast_in_dim.13), channel_id=1, replica_groups=mesh['bank'=16,'zero'=16] {'zero'}, dimensions={0} | all-to-all | bytes 32768 | tf_op jit(solution)/shard_map/all_to_all | solution.py:15
  151.1 6.8 %all-to-all-start.2 = ((bf16[16,2048,4]{1,2,0:T(4,128)(2,1)}), bf16[16,2048,4]{1,2,0:T(4,128)(2,1)S(1)}, u32[]{:S(2)}, u32[]{:S(2)}) async-start(bf16[16,2048,4]{1,2,0:T(4,128)(2,1)} %broadcast_in_dim.14), calls=%async_computation.2 | async-start | bytes 524288 | tf_op jit(solution)/shard_map/all_to_all | solution.py:15
  157.9 8.1 %all-to-all-done.2 = bf16[16,2048,4]{1,2,0:T(4,128)(2,1)S(1)} async-done(((bf16[16,2048,4]{1,2,0:T(4,128)(2,1)}), bf16[16,2048,4]{1,2,0:T(4,128)(2,1)S(1)}, u32[]{:S(2)}, u32[]{:S(2)}) %all-to-all-start.2) | async-done | bytes 262176 | tf_op jit(solution)/shard_map/all_to_all | solution.py:15
  196.0 13.0 %gather_fusion = bf16[16,4,1024,128]{3,2,1,0:T(8,128)(2,1)} fusion(bf16[16,4,1024,128]{3,2,1,0:T(8,128)(2,1)} %bitcast_dynamic-update-slice_fusion, s32[1024]{0:T(1024)S(1)} %pad_clamp_fusion), kind=kCustom, calls=%fused_computation | custom fusion | bytes 33554496 | tf_op jit(solution)/shard_map/gather | solution.py:49
  209.0 14.4 %copy_bitcast_fusion = bf16[4,1024,2048]{2,1,0:T(8,128)(2,1)} fusion(bf16[16,4,1024,128]{3,2,1,0:T(8,128)(2,1)} %gather_fusion), kind=kLoop, calls=%fused_computation.1 | loop fusion | bytes 33554432 | tf_op jit(solution)/shard_map/reshape | solution.py:10
  (63 shorter events, 45.4 us)
Async XLA Ops:
  24.6 168.1 %copy-start.11 = (f32[4,1024]{1,0:T(4,128)}, f32[4,1024]{1,0:T(4,128)S(1)}, u32[]{:S(2)}) copy-start(f32[4,1024]{1,0:T(4,128)S(1)} %sqrt.7) | copy-start | bytes 49156
  26.8 11.8 %collective-permute-start = (bf16[4,1024,128]{2,1,0:T(8,128)(2,1)S(1)}, bf16[4,1024,128]{2,1,0:T(8,128)(2,1)S(1)}, u32[]{:S(2)}, u32[]{:S(2)}) collective-permute-start(bf16[4,1024,128]{2,1,0:T(8,128)(2,1)S(1)} %divide_convert_fusion), channel_id=1, source_target_pairs={{0,1},{1,2},{2,3},{3,4},{4,5},{5,6},{6,7},{7,8},{8,9},{9,10},{10,1... | collective-permute-start | bytes 3145736 | tf_op jit(solution)/shard_map/ppermute | solution.py:44
  38.6 14.2 %collective-permute-start.1 = (bf16[4,1024,128]{2,1,0:T(8,128)(2,1)S(1)}, bf16[4,1024,128]{2,1,0:T(8,128)(2,1)S(1)}, u32[]{:S(2)}, u32[]{:S(2)}) collective-permute-start(bf16[4,1024,128]{2,1,0:T(8,128)(2,1)S(1)} %collective-permute-done), channel_id=1, source_target_pairs={{0,1},{1,2},{2,3},{3,4},{4,5},{5,6},{6,7},{7,8},{8,9},{9,10},{10,1... | collective-permute-start | bytes 3145736 | tf_op jit(solution)/shard_map/ppermute | solution.py:44
  41.1 14.5 %collective-permute-start.8 = (bf16[4,1024,128]{2,1,0:T(8,128)(2,1)S(1)}, bf16[4,1024,128]{2,1,0:T(8,128)(2,1)S(1)}, u32[]{:S(2)}, u32[]{:S(2)}) collective-permute-start(bf16[4,1024,128]{2,1,0:T(8,128)(2,1)S(1)} %divide_convert_fusion), channel_id=1, source_target_pairs={{1,0},{2,1},{3,2},{4,3},{5,4},{6,5},{7,6},{8,7},{9,8},{10,9},{11,1... | collective-permute-start | bytes 3145736 | tf_op jit(solution)/shard_map/ppermute | solution.py:46
  52.8 17.3 %copy-start = (bf16[4,1024,128]{2,1,0:T(8,128)(2,1)}, bf16[4,1024,128]{2,1,0:T(8,128)(2,1)S(1)}, u32[]{:S(2)}) copy-start(bf16[4,1024,128]{2,1,0:T(8,128)(2,1)S(1)} %collective-permute-done.1) | copy-start | bytes 3145732
  52.8 14.2 %collective-permute-start.2 = (bf16[4,1024,128]{2,1,0:T(8,128)(2,1)S(1)}, bf16[4,1024,128]{2,1,0:T(8,128)(2,1)S(1)}, u32[]{:S(2)}, u32[]{:S(2)}) collective-permute-start(bf16[4,1024,128]{2,1,0:T(8,128)(2,1)S(1)} %collective-permute-done.1), channel_id=1, source_target_pairs={{0,1},{1,2},{2,3},{3,4},{4,5},{5,6},{6,7},{7,8},{8,9},{9,10},{10,1... | collective-permute-start | bytes 3145736 | tf_op jit(solution)/shard_map/ppermute | solution.py:44
  55.6 14.5 %collective-permute-start.9 = (bf16[4,1024,128]{2,1,0:T(8,128)(2,1)S(1)}, bf16[4,1024,128]{2,1,0:T(8,128)(2,1)S(1)}, u32[]{:S(2)}, u32[]{:S(2)}) collective-permute-start(bf16[4,1024,128]{2,1,0:T(8,128)(2,1)S(1)} %collective-permute-done.8), channel_id=1, source_target_pairs={{1,0},{2,1},{3,2},{4,3},{5,4},{6,5},{7,6},{8,7},{9,8},{10,9},{11,1... | collective-permute-start | bytes 3145736 | tf_op jit(solution)/shard_map/ppermute | solution.py:46
  67.0 17.6 %copy-start.3 = (bf16[4,1024,128]{2,1,0:T(8,128)(2,1)}, bf16[4,1024,128]{2,1,0:T(8,128)(2,1)S(1)}, u32[]{:S(2)}) copy-start(bf16[4,1024,128]{2,1,0:T(8,128)(2,1)S(1)} %collective-permute-done.2) | copy-start | bytes 3145732
  67.0 14.2 %collective-permute-start.3 = (bf16[4,1024,128]{2,1,0:T(8,128)(2,1)S(1)}, bf16[4,1024,128]{2,1,0:T(8,128)(2,1)S(1)}, u32[]{:S(2)}, u32[]{:S(2)}) collective-permute-start(bf16[4,1024,128]{2,1,0:T(8,128)(2,1)S(1)} %collective-permute-done.2), channel_id=1, source_target_pairs={{0,1},{1,2},{2,3},{3,4},{4,5},{5,6},{6,7},{7,8},{8,9},{9,10},{10,1... | collective-permute-start | bytes 3145736 | tf_op jit(solution)/shard_map/ppermute | solution.py:44
  70.1 14.5 %collective-permute-start.10 = (bf16[4,1024,128]{2,1,0:T(8,128)(2,1)S(1)}, bf16[4,1024,128]{2,1,0:T(8,128)(2,1)S(1)}, u32[]{:S(2)}, u32[]{:S(2)}) collective-permute-start(bf16[4,1024,128]{2,1,0:T(8,128)(2,1)S(1)} %collective-permute-done.9), channel_id=1, source_target_pairs={{1,0},{2,1},{3,2},{4,3},{5,4},{6,5},{7,6},{8,7},{9,8},{10,9},{11,1... | collective-permute-start | bytes 3145736 | tf_op jit(solution)/shard_map/ppermute | solution.py:46
  81.3 33.4 %copy-start.8 = (bf16[4,1024,128]{2,1,0:T(8,128)(2,1)}, bf16[4,1024,128]{2,1,0:T(8,128)(2,1)S(1)}, u32[]{:S(2)}) copy-start(bf16[4,1024,128]{2,1,0:T(8,128)(2,1)S(1)} %collective-permute-done.3) | copy-start | bytes 3145732
  81.3 14.2 %collective-permute-start.4 = (bf16[4,1024,128]{2,1,0:T(8,128)(2,1)S(1)}, bf16[4,1024,128]{2,1,0:T(8,128)(2,1)S(1)}, u32[]{:S(2)}, u32[]{:S(2)}) collective-permute-start(bf16[4,1024,128]{2,1,0:T(8,128)(2,1)S(1)} %collective-permute-done.3), channel_id=1, source_target_pairs={{0,1},{1,2},{2,3},{3,4},{4,5},{5,6},{6,7},{7,8},{8,9},{9,10},{10,1... | collective-permute-start | bytes 3145736 | tf_op jit(solution)/shard_map/ppermute | solution.py:44
  84.6 14.5 %collective-permute-start.11 = (bf16[4,1024,128]{2,1,0:T(8,128)(2,1)S(1)}, bf16[4,1024,128]{2,1,0:T(8,128)(2,1)S(1)}, u32[]{:S(2)}, u32[]{:S(2)}) collective-permute-start(bf16[4,1024,128]{2,1,0:T(8,128)(2,1)S(1)} %collective-permute-done.10), channel_id=1, source_target_pairs={{1,0},{2,1},{3,2},{4,3},{5,4},{6,5},{7,6},{8,7},{9,8},{10,9},{11,1... | collective-permute-start | bytes 3145736 | tf_op jit(solution)/shard_map/ppermute | solution.py:46
  95.5 24.5 %copy-start.9 = (bf16[4,1024,128]{2,1,0:T(8,128)(2,1)}, bf16[4,1024,128]{2,1,0:T(8,128)(2,1)S(1)}, u32[]{:S(2)}) copy-start(bf16[4,1024,128]{2,1,0:T(8,128)(2,1)S(1)} %collective-permute-done.4) | copy-start | bytes 3145732
  95.5 14.2 %collective-permute-start.5 = (bf16[4,1024,128]{2,1,0:T(8,128)(2,1)S(1)}, bf16[4,1024,128]{2,1,0:T(8,128)(2,1)S(1)}, u32[]{:S(2)}, u32[]{:S(2)}) collective-permute-start(bf16[4,1024,128]{2,1,0:T(8,128)(2,1)S(1)} %collective-permute-done.4), channel_id=1, source_target_pairs={{0,1},{1,2},{2,3},{3,4},{4,5},{5,6},{6,7},{7,8},{8,9},{9,10},{10,1... | collective-permute-start | bytes 3145736 | tf_op jit(solution)/shard_map/ppermute | solution.py:44
  100.1 14.5 %collective-permute-start.12 = (bf16[4,1024,128]{2,1,0:T(8,128)(2,1)S(1)}, bf16[4,1024,128]{2,1,0:T(8,128)(2,1)}, u32[]{:S(2)}, u32[]{:S(2)}) collective-permute-start(bf16[4,1024,128]{2,1,0:T(8,128)(2,1)S(1)} %collective-permute-done.11), channel_id=1, source_target_pairs={{1,0},{2,1},{3,2},{4,3},{5,4},{6,5},{7,6},{8,7},{9,8},{10,9},{11,1... | collective-permute-start | bytes 3145736 | tf_op jit(solution)/shard_map/ppermute | solution.py:46
  109.7 14.2 %collective-permute-start.6 = (bf16[4,1024,128]{2,1,0:T(8,128)(2,1)S(1)}, bf16[4,1024,128]{2,1,0:T(8,128)(2,1)}, u32[]{:S(2)}, u32[]{:S(2)}) collective-permute-start(bf16[4,1024,128]{2,1,0:T(8,128)(2,1)S(1)} %collective-permute-done.5), channel_id=1, source_target_pairs={{0,1},{1,2},{2,3},{3,4},{4,5},{5,6},{6,7},{7,8},{8,9},{9,10},{10,1... | collective-permute-start | bytes 3145736 | tf_op jit(solution)/shard_map/ppermute | solution.py:44
  114.7 52.1 %collective-permute-start.13 = (bf16[4,1024,128]{2,1,0:T(8,128)(2,1)}, bf16[4,1024,128]{2,1,0:T(8,128)(2,1)}, u32[]{:S(2)}, u32[]{:S(2)}) collective-permute-start(bf16[4,1024,128]{2,1,0:T(8,128)(2,1)} %collective-permute-done.12), channel_id=1, source_target_pairs={{1,0},{2,1},{3,2},{4,3},{5,4},{6,5},{7,6},{8,7},{9,8},{10,9},{11,1... | collective-permute-start | bytes 3145736 | tf_op jit(solution)/shard_map/ppermute | solution.py:46
  124.0 44.4 %collective-permute-start.7 = (bf16[4,1024,128]{2,1,0:T(8,128)(2,1)}, bf16[4,1024,128]{2,1,0:T(8,128)(2,1)}, u32[]{:S(2)}, u32[]{:S(2)}) collective-permute-start(bf16[4,1024,128]{2,1,0:T(8,128)(2,1)} %collective-permute-done.6), channel_id=1, source_target_pairs={{0,1},{1,2},{2,3},{3,4},{4,5},{5,6},{6,7},{7,8},{8,9},{9,10},{10,1... | collective-permute-start | bytes 3145736 | tf_op jit(solution)/shard_map/ppermute | solution.py:44
  151.1 14.9 %all-to-all-start.2 = ((bf16[16,2048,4]{1,2,0:T(4,128)(2,1)}), bf16[16,2048,4]{1,2,0:T(4,128)(2,1)S(1)}, u32[]{:S(2)}, u32[]{:S(2)}) async-start(bf16[16,2048,4]{1,2,0:T(4,128)(2,1)} %broadcast_in_dim.14), calls=%async_computation.2 | async-start | bytes 524288 | tf_op jit(solution)/shard_map/all_to_all | solution.py:15
  166.8 20.5 %copy-start.2 = (bf16[4,1024,128]{2,1,0:T(8,128)(2,1)S(1)}, bf16[4,1024,128]{2,1,0:T(8,128)(2,1)}, u32[]{:S(2)}) copy-start(bf16[4,1024,128]{2,1,0:T(8,128)(2,1)} %copy-done.1) | copy-start | bytes 3145732
  166.8 21.5 %copy-start.5 = (bf16[4,1024,128]{2,1,0:T(8,128)(2,1)S(1)}, bf16[4,1024,128]{2,1,0:T(8,128)(2,1)}, u32[]{:S(2)}) copy-start(bf16[4,1024,128]{2,1,0:T(8,128)(2,1)} %copy-done.4) | copy-start | bytes 3145732
  166.8 22.6 %copy-start.7 = (bf16[4,1024,128]{2,1,0:T(8,128)(2,1)S(1)}, bf16[4,1024,128]{2,1,0:T(8,128)(2,1)}, u32[]{:S(2)}) copy-start(bf16[4,1024,128]{2,1,0:T(8,128)(2,1)} %copy-done.6) | copy-start | bytes 3145732
  166.8 28.1 %collective-permute-start.14 = (bf16[4,1024,128]{2,1,0:T(8,128)(2,1)}, bf16[4,1024,128]{2,1,0:T(8,128)(2,1)S(1)}, u32[]{:S(2)}, u32[]{:S(2)}) collective-permute-start(bf16[4,1024,128]{2,1,0:T(8,128)(2,1)} %collective-permute-done.13), channel_id=1, source_target_pairs={{1,0},{2,1},{3,2},{4,3},{5,4},{6,5},{7,6},{8,7},{9,8},{10,9},{11,1... | collective-permute-start | bytes 3145736 | tf_op jit(solution)/shard_map/ppermute | solution.py:46
  (4 other events, 21.6 us)
